TPU v7x, 32 devices: a whole 2x2x4 slice. The times are simulated.
32 devices in a mesh: groups: 2 (over x), tile: 16 (over z, y, core).
Axes of the slice: x: 2, y: 2, z: 4, core: 2. Of those that a mesh axis runs over, the one named last changes fastest.
Arguments:
- echoes: float32 [2, 32, 16384], P(None, ('groups', 'tile')), parts along dimension 1, may hold values from -6 to 6
- bin_start: int32 [32, 16], P(('groups', 'tile')), parts along dimension 0, may hold values from 0 to 16128
- bin_fraction: float32 [16, 32], P(None, ('groups', 'tile')), parts along dimension 1, may hold values from 0 to 1
- row_phase: float32 [16, 32, 128], P(None, ('groups', 'tile')), parts along dimension 1, may hold values from -3.140625 to 3.140625
- column_phase: float32 [16, 32, 128], P(None, ('groups', 'tile')), parts along dimension 1, may hold values from -3.140625 to 3.140625
- row_bin: int32 [16, 32, 128], P(None, ('groups', 'tile')), parts along dimension 1, may hold values from 0 to 127
- column_bin: int32 [16, 32, 128], P(None, ('groups', 'tile')), parts along dimension 1, may hold values from 0 to 127
Outputs:
- focused: float32 [2, 32, 128, 128], P(None, ('groups', 'tile')), parts along dimension 1
- correction: float32 [2, 32], P(None, ('groups', 'tile')), parts along dimension 1
There are 2 independent parts, one for each index of `groups`. A program takes and returns all parts, laid end to end along the dimension named above; each array names one. Nothing has to cross between parts.
Inputs may be any that keep to these rules, and one draw needn't show every extreme that they name: The window of 256 range bins that begins at bin_start lies within the 16384 bins.
All inputs are finite; a program needn't handle non-finite values.
Results may differ from a plain program's by a relative error of at most 0.012.
Values may be sent and summed in bfloat16 or wider, within the bound.
A program may use at most 320 MiB of HBM per device.

v0:
```python
import math

import jax
import jax.numpy as jnp
from jax import lax
from jax.sharding import PartitionSpec as P

ROWS = 128
COLS = 128
BINR = 128
BINC = 128


highest = lax.Precision.HIGHEST
pulse_group = 16


def rounded(values):
    return lax.optimization_barrier(values.astype(jnp.bfloat16)).astype(jnp.float32)


def normalize(real_part, imag_part):
    magnitude = real_part * real_part + imag_part * imag_part
    denominator = jnp.sqrt(magnitude + jnp.mean(magnitude) + 1e-06)
    return (real_part / denominator, imag_part / denominator)


def twiddle(row_count, column_count, period):
    product = (
        jnp.arange(row_count, dtype=jnp.int32)[:, None]
        * jnp.arange(column_count, dtype=jnp.int32)[None, :]
        % period
    )
    phases = product.astype(jnp.float32) * (2.0 * math.pi / period)
    return (jnp.cos(phases), jnp.sin(phases))


def apply_table(pattern, tables, real_part, imag_part):
    cosine_table, sine_table = tables
    new_real = jnp.einsum(pattern, cosine_table, real_part, precision=highest) + jnp.einsum(
        pattern, sine_table, imag_part, precision=highest
    )
    new_imag = jnp.einsum(pattern, cosine_table, imag_part, precision=highest) - jnp.einsum(
        pattern, sine_table, real_part, precision=highest
    )
    return (new_real, new_imag)


def compress(echoes):
    samples = echoes.shape[2]
    inner_len = 128
    outer_len = samples // inner_len
    signal_real = echoes[0].reshape(-1, outer_len, inner_len)
    signal_imag = echoes[1].reshape(-1, outer_len, inner_len)
    section_real, section_imag = apply_table(
        "kb,pba->pka", twiddle(outer_len, outer_len, outer_len), signal_real, signal_imag
    )
    cosine_table, sine_table = twiddle(outer_len, inner_len, samples)
    turned_real = section_real * cosine_table + section_imag * sine_table
    turned_imag = section_imag * cosine_table - section_real * sine_table
    final_real, final_imag = apply_table(
        "an,pkn->pak", twiddle(inner_len, inner_len, inner_len), turned_real, turned_imag
    )
    norm_scale = 1.0 / math.sqrt(samples)
    stacked = jnp.stack(
        [
            final_real.reshape(-1, samples) * norm_scale,
            final_imag.reshape(-1, samples) * norm_scale,
        ],
        axis=1,
    )
    return stacked.astype(jnp.bfloat16)


def per_device(echoes, bin_start, bin_fraction, row_phase, column_phase, row_bin, column_bin):
    spectra = compress(echoes)
    window_len = BINR + BINC

    def cut_window(profile, offset):
        return lax.dynamic_slice_in_dim(profile, offset, window_len, 1)

    outgoing = jax.vmap(
        lambda profile, begins: jax.vmap(lambda offset: cut_window(profile, offset))(begins)
    )(spectra, bin_start)
    gathered = lax.all_to_all(outgoing, "tile", split_axis=1, concat_axis=0, tiled=True)[:, 0]
    pulses = gathered.shape[0]
    fractions = bin_fraction[:, 0]
    row_angles = row_phase[:, 0]
    row_bins = row_bin[:, 0]
    column_angles = column_phase[:, 0]
    column_bins = column_bin[:, 0]
    blocks = pulses // pulse_group
    block_ids = jnp.arange(blocks, dtype=jnp.int32)
    norm_scale = 1.0 / math.sqrt(pulses)
    bin_rows = jnp.arange(BINR, dtype=jnp.int32)
    bin_columns = jnp.arange(BINC, dtype=jnp.int32)

    def take_block(values, block_index):
        return lax.dynamic_slice_in_dim(values, block_index * pulse_group, pulse_group, 0)

    def contribution(block_index):
        window = take_block(gathered, block_index).astype(jnp.float32)
        weight_frac = take_block(fractions, block_index)[:, None, None]
        profile = ((1.0 - weight_frac) * window[..., :-1] + weight_frac * window[..., 1:]).astype(
            jnp.bfloat16
        )
        length = profile.shape[-1]
        repeated = jnp.tile(profile, (1, 1, BINR + 1))[..., : BINR * (length + 1)]
        hankel = repeated.reshape(pulse_group, 2, BINR, length + 1)[..., :BINC]
        pick_rows = (take_block(row_bins, block_index)[:, :, None] == bin_rows).astype(jnp.bfloat16)
        chosen = jnp.einsum("pur,pxrc->pxuc", pick_rows, hankel, preferred_element_type=jnp.float32)
        angles = take_block(row_angles, block_index)[:, :, None]
        row_cosine = rounded(jnp.cos(angles))
        row_sine = rounded(jnp.sin(angles))
        steered = jnp.stack(
            [
                row_cosine * chosen[:, 0] - row_sine * chosen[:, 1],
                row_cosine * chosen[:, 1] + row_sine * chosen[:, 0],
            ],
            1,
        ).astype(jnp.bfloat16)
        pick_columns = (take_block(column_bins, block_index)[:, :, None] == bin_columns).astype(
            jnp.bfloat16
        )
        selected = jnp.einsum(
            "pxuc,pvc->pxuv", steered, pick_columns, preferred_element_type=jnp.float32
        )
        angles = take_block(column_angles, block_index)[:, None, :]
        column_cosine = rounded(jnp.cos(angles))
        column_sine = rounded(jnp.sin(angles))
        return (
            column_cosine * selected[:, 0] - column_sine * selected[:, 1],
            column_cosine * selected[:, 1] + column_sine * selected[:, 0],
        )

    stored_real, stored_imag = lax.map(contribution, block_ids)
    part_real = stored_real.reshape(pulses, ROWS, COLS)
    part_imag = stored_imag.reshape(pulses, ROWS, COLS)

    def image_of(weight_real, weight_imag):
        image_real = jnp.tensordot(weight_real, part_real, 1, precision=highest) - jnp.tensordot(
            weight_imag, part_imag, 1, precision=highest
        )
        image_imag = jnp.tensordot(weight_real, part_imag, 1, precision=highest) + jnp.tensordot(
            weight_imag, part_real, 1, precision=highest
        )
        return (image_real * norm_scale, image_imag * norm_scale)

    def correlate(image_real, image_imag):
        return (
            jnp.sum(part_real * image_real + part_imag * image_imag, axis=(1, 2)),
            jnp.sum(part_real * image_imag - part_imag * image_real, axis=(1, 2)),
        )

    energy = jnp.sum(part_real * part_real + part_imag * part_imag, axis=(1, 2))
    unit_weights = jnp.ones((pulses,), jnp.float32)
    zero_weights = jnp.zeros((pulses,), jnp.float32)
    first_real, first_imag = image_of(unit_weights, zero_weights)
    cross_real, cross_imag = correlate(first_real, first_imag)
    cross_real, cross_imag, energy = lax.psum((cross_real, cross_imag, energy), "tile")
    one_real, one_imag = normalize(cross_real - energy * norm_scale, cross_imag)
    second_real, second_imag = image_of(one_real, one_imag)
    cross_real, cross_imag = correlate(second_real, second_imag)
    cross_real, cross_imag = lax.psum((cross_real, cross_imag), "tile")
    rest_real = cross_real - one_real * energy * norm_scale
    rest_imag = cross_imag - one_imag * energy * norm_scale
    again_real = one_real * rest_real + one_imag * rest_imag
    again_imag = one_real * rest_imag - one_imag * rest_real
    two_real, two_imag = normalize(again_real, again_imag)
    total_real = one_real * two_real - one_imag * two_imag
    total_imag = one_real * two_imag + one_imag * two_real
    final_real, final_imag = image_of(total_real, total_imag)
    focused = jnp.stack([final_real, final_imag])[:, None]
    own_pulses = echoes.shape[1]
    first_pulse = lax.axis_index("tile") * own_pulses
    correction = lax.dynamic_slice_in_dim(
        jnp.stack([total_real, total_imag]), first_pulse, own_pulses, 1
    )
    return (focused, correction)


def solution(mesh):
    in_specs = (
        P(None, ("groups", "tile"), None),
        P(("groups", "tile"), None),
        P(None, ("groups", "tile")),
        P(None, ("groups", "tile"), None),
        P(None, ("groups", "tile"), None),
        P(None, ("groups", "tile"), None),
        P(None, ("groups", "tile"), None),
    )
    out_specs = (P(None, ("groups", "tile"), None, None), P(None, ("groups", "tile")))
    return jax.shard_map(
        per_device, mesh=mesh, in_specs=in_specs, out_specs=out_specs, check_vma=False
    )
```

profile of v0, /device:TPU:0, one launch (start us, length us, event | category | flops | bytes accessed | tf_op | source)
XLA Modules:
  0.0 126.8 jit_solution(10631370937224454987)
XLA Ops:
  0.6 0.9 fusion.147
  1.5 0.4 fusion.69
  2.0 0.4 fusion.71
  2.4 0.5 fusion.2
  2.9 0.5 fusion.3
  3.4 0.7 fusion.53
  4.1 0.7 fusion.49
  4.8 0.7 fusion.7
  5.5 0.1 copy.31
  5.7 0.7 fusion.6
  6.4 0.1 copy.32
  6.6 0.2 pad_maximum_fusion
  6.7 0.0 copy-start.5
  6.8 0.0 copy-start.2
  6.8 0.0 copy-start.3
  6.8 0.0 copy-start.4
  6.8 12.8 %copy.33 = bf16[1,2,16384]{1,0,2:T(2,128)(2,1)} copy(bf16[1,2,16384]{2,1,0:T(2,128)(2,1)S(1)} %pad_maximum_fusion) | data formatting | bytes 131072 | tf_op jit(solution)/shard_map/stack | solution.py:65
  19.6 0.0 copy-done.5
  19.6 3.8 %gather_fusion = bf16[16,2,256]{1,0,2:T(8,128)(2,1)S(1)} fusion(bf16[1,2,16384]{1,0,2:T(2,128)(2,1)} %copy.33, s32[16]{0:T(128)S(1)} %or_bitcast_fusion), kind=kCustom, calls=%fused_computation | custom fusion | bytes 32960 | tf_op jit(solution)/shard_map/vmap(vmap())/gather | solution.py:80
  23.4 1.5 %copy.34 = bf16[1,16,2,256]{3,2,0,1:T(2,128)(2,1)} copy(bf16[1,16,2,256]{2,1,3,0:T(8,128)(2,1)S(1)} %bitcast.154) | data formatting | bytes 32768 | tf_op jit(solution)/shard_map/vmap(vmap())/gather | solution.py:80
  24.9 7.4 %all-to-all-start = ((bf16[1,16,2,256]{3,2,0,1:T(2,128)(2,1)}), bf16[1,16,2,256]{3,2,0,1:T(2,128)(2,1)S(1)}, u32[]{:S(2)}, u32[]{:S(2)}) async-start(bf16[1,16,2,256]{3,2,0,1:T(2,128)(2,1)} %copy.34), calls=%async_computation | async-start | bytes 32768 | tf_op jit(solution)/shard_map/all_to_all | solution.py:85
  32.3 0.0 copy-done.2
  32.3 0.2 cosine_convert_fusion
  32.6 0.0 copy-done.3
  32.6 0.2 cosine_convert_fusion.1
  32.9 0.0 copy-done.4
  32.9 5.9 %all-to-all-done = bf16[1,16,2,256]{3,2,0,1:T(2,128)(2,1)S(1)} async-done(((bf16[1,16,2,256]{3,2,0,1:T(2,128)(2,1)}), bf16[1,16,2,256]{3,2,0,1:T(2,128)(2,1)S(1)}, u32[]{:S(2)}, u32[]{:S(2)}) %all-to-all-start) | async-done | bytes 16416 | tf_op jit(solution)/shard_map/all_to_all | solution.py:85
  38.8 0.1 fusion.62
  38.9 0.2 tile.15
  39.1 3.3 %tile.16 = bf16[16,2,32895]{2,0,1:T(8,128)(2,1)} reshape(bf16[16,2,129,255]{3,2,0,1:T(8,128)(2,1)S(1)} %tile.15) | data formatting | bytes 4210560 | tf_op jit(solution)/shard_map/while/body/eval_jaxpr/tile | solution.py:108
  42.3 0.0 slice-start
  42.3 1.6 %slice-done = bf16[16,2,32768]{2,0,1:T(8,128)(2,1)S(1)} async-done(((bf16[16,2,32895]{2,0,1:T(8,128)(2,1)}), bf16[16,2,32768]{2,0,1:T(8,128)(2,1)S(1)}, s32[]{:S(2)}) %slice-start) | async-done | bytes 2097176 | tf_op jit(solution)/shard_map/while/body/eval_jaxpr/slice | solution.py:108
  43.9 0.0 copy-start
  43.9 0.5 copy.61
  44.4 0.2 copy-done
  44.6 1.0 convolution_bitcast_fusion
  45.6 0.0 copy-start.1
  45.6 0.3 subtract_convert_fusion
  46.0 0.4 copy-done.1
  46.3 1.5 %fusion.8 = f32[16,2,128,128]{3,2,1,0:T(8,128)S(1)} fusion(bf16[16,1,128,128]{2,3,1,0:T(8,128)(2,1)S(1)} %get-tuple-element.85, bf16[16,1,128,128]{2,3,1,0:T(8,128)(2,1)S(1)} %get-tuple-element.84, s32[16,128]{1,0:T(8,128)S(1)} %bitcast.174), kind=kOutput, calls=%fused_computation.16 | convolution fusion | flops 135004160 | bytes 3153920 | tf_op jit(solution)/shard_map/while/body/eval_jaxpr/pxuc,pvc->pxuv/dot_general | solution.py:125
  47.8 0.4 multiply_subtract_fusion
  48.2 1.2 fusion.27
  49.3 1.2 fusion.25
  50.5 1.2 fusion.39
  51.7 1.2 fusion.37
  52.9 0.6 add_reduce_fusion.2
  53.5 29.9 %all-reduce.2 = (f32[16]{0:T(128)S(1)}, f32[16]{0:T(128)S(1)}, f32[16]{0:T(128)S(1)}) all-reduce(f32[16]{0:T(128)S(1)} %get-tuple-element.67, f32[16]{0:T(128)S(1)} %get-tuple-element.66, f32[16]{0:T(128)S(1)} %get-tuple-element.68), channel_id=1, replica_groups=mesh['groups'=2,'tile'=16] {'tile'}, use_global_device_ids=true, to_apply=%region_5.6 | all-reduce | flops 48 | bytes 384 | tf_op jit(solution)/shard_map/psum | solution.py:160
  83.4 0.6 fusion.146
  84.7 1.2 fusion.23
  85.9 1.2 fusion.33
  87.1 1.2 fusion.35
  88.2 1.2 fusion.21
  89.5 0.4 subtract_reduce_fusion
  89.9 29.5 %all-reduce.1 = (f32[16]{0:T(128)S(1)}, f32[16]{0:T(128)S(1)}) all-reduce(f32[16]{0:T(128)S(1)} %get-tuple-element.65, f32[16]{0:T(128)S(1)} %get-tuple-element.64), channel_id=1, replica_groups=mesh['groups'=2,'tile'=16] {'tile'}, use_global_device_ids=true, to_apply=%region_8.9 | all-reduce | flops 32 | bytes 256 | tf_op jit(solution)/shard_map/psum | solution.py:164
  119.4 0.6 fusion.143
  120.6 1.2 fusion.19
  121.8 1.2 fusion.29
  123.0 1.2 fusion.31
  124.2 1.2 fusion.17
  125.4 0.1 constant_dynamic-slice_fusion
  125.5 0.6 copy.39
  126.1 0.7 maximum_bitcast_fusion
  (22 shorter events, 0.2 us)
Async XLA Ops:
  6.7 12.9 %copy-start.5 = (s32[1,16]{1,0:T(1,128)S(1)}, s32[1,16]{1,0:T(1,128)}, u32[]{:S(2)}) copy-start(s32[1,16]{1,0:T(1,128)} %param.8) | copy-start | bytes 196
  6.8 25.6 %copy-start.2 = (f32[16,1,128]{2,1,0:T(1,128)S(1)}, f32[16,1,128]{2,1,0:T(1,128)}, u32[]{:S(2)}) copy-start(f32[16,1,128]{2,1,0:T(1,128)} %param.10) | copy-start | bytes 24580
  6.8 25.9 %copy-start.3 = (f32[16,1,128]{2,1,0:T(1,128)S(1)}, f32[16,1,128]{2,1,0:T(1,128)}, u32[]{:S(2)}) copy-start(f32[16,1,128]{2,1,0:T(1,128)} %param.11) | copy-start | bytes 24580
  6.8 26.1 %copy-start.4 = (f32[16,1]{0,1:T(1,128)S(1)}, f32[16,1]{0,1:T(1,128)}, u32[]{:S(2)}) copy-start(f32[16,1]{0,1:T(1,128)} %param.9) | copy-start | bytes 196
  24.9 13.9 %all-to-all-start = ((bf16[1,16,2,256]{3,2,0,1:T(2,128)(2,1)}), bf16[1,16,2,256]{3,2,0,1:T(2,128)(2,1)S(1)}, u32[]{:S(2)}, u32[]{:S(2)}) async-start(bf16[1,16,2,256]{3,2,0,1:T(2,128)(2,1)} %copy.34), calls=%async_computation | async-start | bytes 32768 | tf_op jit(solution)/shard_map/all_to_all | solution.py:85
  42.3 1.6 %slice-start = ((bf16[16,2,32895]{2,0,1:T(8,128)(2,1)}), bf16[16,2,32768]{2,0,1:T(8,128)(2,1)S(1)}, s32[]{:S(2)}) async-start(bf16[16,2,32895]{2,0,1:T(8,128)(2,1)} %tile.16), calls=%async_computation.1 | async-start | bytes 4194304 | tf_op jit(solution)/shard_map/while/body/eval_jaxpr/slice | solution.py:108
  43.9 0.7 copy-start
  45.6 0.7 copy-start.1
where the time goes:
time: 127 us
  blocking collectives  59.4 us (47%)
  local copies, waits for them, and re-layouts  26 us (20%)
  matrix products  21.3 us (17%)
  starting transfers between devices  7.42 us (6%)
  waiting for transfers between devices  5.88 us (5%)
  other arithmetic  4.44 us (3%)
  between operations  2.38 us (2%)
    psum x1, blocking collectives, per_device(): lax.psum((cross_real, cross_imag, energy), 'tile')  29.9 us
    psum x1, blocking collectives, per_device(): cross_real, cross_imag = lax.psum((cross_real, cross_imag), 'tile')  29.5 us
    another operation x3, local copies, waits for them, and re-layouts, compress(): jnp.stack([final_real.reshape(-1, samples) * norm_scale, final_imag.resha...  12.9 us
    all_to_all x1, starting transfers between devices, per_device(): lax.all_to_all(outgoing, 'tile', split_axis=1, concat_axis=0, tiled=True)  7.42 us
    all_to_all x1, waiting for transfers between devices, per_device(): lax.all_to_all(outgoing, 'tile', split_axis=1, concat_axis=0, tiled=True)  5.88 us
    gather x3, local copies, waits for them, and re-layouts, cut_window(): return lax.dynamic_slice_in_dim(profile, offset, window_len, 1)  5.26 us
    dot_general x3, matrix products, image_of(): jnp.tensordot(weight_imag, part_imag, 1, precision=highest)  3.54 us
    dot_general x3, matrix products, image_of(): jnp.tensordot(weight_real, part_imag, 1, precision=highest)  3.53 us
  transfers between devices with their start and end apart: 1, of which 1 were waited for; matrix products, arithmetic and copies ran while one was open for 0% of the time, Pallas kernels for 0%

commit v1 on v0

v1 whole, which is shorter than its diff:
```python
import functools
import math

import jax
import jax.numpy as jnp
import numpy as np
from jax import lax
from jax.experimental import pallas as pl
from jax.experimental.pallas import tpu as pltpu
from jax.sharding import PartitionSpec as P

LANES = 128
OCTET = 8
MESH = pl.DeviceIdType.MESH
F32 = jnp.float32
BF16 = jnp.bfloat16


def tables(samples):
    inner = LANES
    outer = samples // inner

    def wave(rows, columns, period):
        product = np.arange(rows)[:, None] * np.arange(columns)[None, :] % period
        phases = product * (2.0 * np.pi / period)
        return np.cos(phases), np.sin(phases)

    def split(table):
        table = table.astype(np.float32)
        high = table.astype(jnp.bfloat16)
        low = (table - high.astype(np.float32)).astype(jnp.bfloat16)
        return np.stack([high, low])

    first = split(np.concatenate(wave(outer, outer, outer), 1))
    last = split(np.concatenate(wave(inner, inner, inner), 1))
    turn = np.stack(wave(outer, inner, samples)) / math.sqrt(samples)
    return first, turn.astype(np.float32), last


def fold_table(pulses):
    block = np.arange(pulses * 2 * OCTET) // OCTET
    pulse, part = block // 2, block % 2
    lane = np.arange(LANES)
    same = [(lane[None, :] == pulse[:, None] + shift * pulses) for shift in (0, 1)]
    real_in = part[:, None] == 0
    real_rows = (same[0] & real_in) * 1.0 + (same[1] & ~real_in) * 1.0
    imag_rows = (same[0] & ~real_in) * 1.0 - (same[1] & real_in) * 1.0
    return np.stack([real_rows, imag_rows]).astype(np.float32)


def dot(a, b, dims=((1,), (0,)), precision=None):
    return lax.dot_general(a, b, (dims, ((), ())), precision=precision, preferred_element_type=F32)


def split3(table_ref, data, dims):
    high = data.astype(BF16)
    low = (data - high.astype(F32)).astype(BF16)
    return dot(table_ref[0], high, dims) + (dot(table_ref[1], high, dims) + dot(table_ref[0], low, dims))


def normalize(real_part, imag_part, axis, count):
    magnitude = real_part * real_part + imag_part * imag_part
    mean = jnp.sum(magnitude, axis=axis, keepdims=True) / count
    denominator = jnp.sqrt(magnitude + mean + 1e-06)
    return real_part / denominator, imag_part / denominator


def kernel(
    n, starts, echo, fraction, row_phase, column_phase, row_bin, column_bin, first, turn, last, fold,
    focused, correction,
    spec, outgoing, gathered, steer, parts, gram_in, message, messages, weights,
    send_sem, recv_sem, send_sem2, recv_sem2,
):
    me = lax.axis_index("tile")
    rows = row_phase.shape[2]
    scale = 1.0 / math.sqrt(n)

    barrier = pltpu.get_barrier_semaphore()
    for k in range(1, n):
        pl.semaphore_signal(barrier, inc=1, device_id={"tile": lax.rem(me + k, n)}, device_id_type=MESH)

    real, imag = echo[0], echo[1]
    data = jnp.concatenate(
        [jnp.concatenate([real, imag], 1), jnp.concatenate([imag, -real], 1)], 0
    )
    section = split3(first, data, ((1,), (0,)))
    half = section.shape[1] // 2
    real, imag = section[:, :half], section[:, half:]
    turned_real = real * turn[0] + imag * turn[1]
    turned_imag = imag * turn[0] - real * turn[1]
    data = jnp.concatenate(
        [jnp.concatenate([turned_real, turned_imag], 1), jnp.concatenate([turned_imag, -turned_real], 1)], 0
    )
    spectrum = split3(last, data, ((1,), (1,)))
    bins = spectrum.shape[0]
    spectrum = spectrum.astype(BF16).astype(F32)
    for h in range(2):
        spec[h, 0:bins, :] = spectrum[:, h * LANES : (h + 1) * LANES]
        spec[h, bins:, :] = jnp.zeros((spec.shape[1] - bins, LANES), F32)

    lane = lax.broadcasted_iota(jnp.int32, (OCTET, LANES), 1)
    for t in range(n):
        start = starts[0, t]
        top = start // LANES
        left = LANES - start % LANES
        pieces = []
        for h in range(2):
            moved = pltpu.roll(spec[h, pl.ds(top, OCTET), :], left % LANES, 1)
            below = pltpu.roll(moved, OCTET - 1, 0)
            pieces.append(jnp.where(lane < left, moved, below)[0:2])
        outgoing[t] = jnp.concatenate(pieces, 0).astype(BF16)

    pl.semaphore_wait(barrier, n - 1)

    def window_copy(k):
        target = lax.rem(me + k, n)
        return pltpu.make_async_remote_copy(
            src_ref=outgoing.at[target],
            dst_ref=gathered.at[me],
            send_sem=send_sem.at[k],
            recv_sem=recv_sem.at[k],
            device_id={"tile": target},
            device_id_type=MESH,
        )

    copies = [window_copy(k) for k in range(1, n)]
    for copy in copies:
        copy.start()
    gathered[me] = outgoing[me]

    def rounded(values):
        return values.astype(BF16).astype(F32)

    angles = row_phase[:, 0, :]
    left_side = jnp.concatenate(
        [
            rounded(jnp.cos(angles)),
            rounded(jnp.sin(angles)),
            row_bin[:, 0, :].astype(F32),
            jnp.ones((n, rows), F32),
        ],
        0,
    )
    left_side = left_side.T.astype(BF16)
    angles = column_phase[:, 0, :]
    cosine, sine = rounded(jnp.cos(angles)), rounded(jnp.sin(angles))
    zero, one = jnp.zeros((n, LANES), F32), jnp.ones((n, LANES), F32)
    right_side = jnp.concatenate(
        [
            jnp.concatenate([cosine, sine, zero], 1),
            jnp.concatenate([-sine, cosine, zero], 1),
            jnp.concatenate([zero, zero, one], 1),
            jnp.concatenate([zero, zero, column_bin[:, 0, :].astype(F32)], 1),
        ],
        0,
    )
    owner = lax.rem(lax.broadcasted_iota(jnp.int32, right_side.shape, 0), n)
    for p in range(n):
        steer[p] = dot(left_side, jnp.where(owner == p, right_side, 0.0).astype(BF16))

    for copy in copies:
        copy.wait()

    lane4 = lax.broadcasted_iota(jnp.int32, (4, LANES), 1)
    for p in range(n):
        window = gathered[p].astype(F32)
        moved = pltpu.roll(window, LANES - 1, 1)
        below = jnp.concatenate([moved[1:4], moved[0:1]], 0)
        shifted = jnp.where(lane4 == LANES - 1, below, moved)
        share = fraction[p : p + 1, 0:1]
        profile = ((1.0 - share) * window + share * shifted).astype(BF16).astype(F32)
        index = steer[p, :, 2 * LANES :].astype(jnp.int32)
        low = index < LANES
        index = index & (LANES - 1)

        def pick(row):
            source = jnp.broadcast_to(profile[row : row + 1, :], (rows, LANES))
            return jnp.take_along_axis(source, index, axis=1, mode="promise_in_bounds")

        real = jnp.where(low, pick(0), pick(1))
        imag = jnp.where(low, pick(2), pick(3))
        turn_real, turn_imag = steer[p, :, :LANES], steer[p, :, LANES : 2 * LANES]
        part_real = turn_real * real - turn_imag * imag
        part_imag = turn_real * imag + turn_imag * real
        parts[p, 0] = part_real
        parts[p, 1] = part_imag
        for t in range(rows // OCTET):
            pair = jnp.concatenate(
                [part_real[t * OCTET : (t + 1) * OCTET], part_imag[t * OCTET : (t + 1) * OCTET]], 0
            )
            gram_in[p * 2 * OCTET : (p + 1) * 2 * OCTET, t * LANES : (t + 1) * LANES] = pair.astype(BF16)

    values = gram_in[...]
    product = dot(values, values, ((1,), (1,)))
    row_id = lax.broadcasted_iota(jnp.int32, product.shape, 0)
    column_id = lax.broadcasted_iota(jnp.int32, product.shape, 1)
    product = jnp.where(lax.rem(row_id, OCTET) == lax.rem(column_id, OCTET), product, 0.0)
    product = product.reshape(n, 2, OCTET, product.shape[1])
    gram = dot(jnp.sum(product[:, 0], axis=1), fold[0], precision=lax.Precision.HIGHEST)
    gram = gram + dot(jnp.sum(product[:, 1], axis=1), fold[1], precision=lax.Precision.HIGHEST)
    groups = LANES // (2 * n)
    depth = n // groups
    packed = gram[0:depth]
    for g in range(1, groups):
        packed = packed + pltpu.roll(gram[g * depth : (g + 1) * depth], g * 2 * n, 1)
    message[...] = packed
    messages[me] = packed

    def gram_copy(k):
        return pltpu.make_async_remote_copy(
            src_ref=message,
            dst_ref=messages.at[me],
            send_sem=send_sem2.at[k],
            recv_sem=recv_sem2.at[k],
            device_id={"tile": lax.rem(me + k, n)},
            device_id_type=MESH,
        )

    copies = [gram_copy(k) for k in range(1, n)]
    for copy in copies:
        copy.start()
    for copy in copies:
        copy.wait()

    total = jnp.sum(messages[...], axis=0)
    gram = jnp.concatenate(
        [total] + [pltpu.roll(total, LANES - g * 2 * n, 1) for g in range(1, groups)], 0
    )
    row_id = lax.broadcasted_iota(jnp.int32, gram.shape, 0)
    column_id = lax.broadcasted_iota(jnp.int32, gram.shape, 1)
    off_diagonal = (column_id < n) & (column_id != row_id)
    gram_real = jnp.where(off_diagonal, gram * scale, 0.0)
    gram_imag = jnp.where(off_diagonal, pltpu.roll(gram, LANES - n, 1) * scale, 0.0)

    def along(values, axis):
        return jnp.sum(values, axis=axis, keepdims=True)

    one_real, one_imag = normalize(along(gram_real, 1), along(gram_imag, 1), 0, n)
    row_real, row_imag = normalize(along(gram_real, 0), -along(gram_imag, 0), 1, n)
    rest_real = along(gram_real * row_real - gram_imag * row_imag, 1)
    rest_imag = along(gram_real * row_imag + gram_imag * row_real, 1)
    again_real = one_real * rest_real + one_imag * rest_imag
    again_imag = one_real * rest_imag - one_imag * rest_real
    two_real, two_imag = normalize(again_real, again_imag, 0, n)
    total_real = one_real * two_real - one_imag * two_imag
    total_imag = one_real * two_imag + one_imag * two_real
    mine = lax.broadcasted_iota(jnp.int32, total_real.shape, 0) == me
    correction[0:1, :] = along(jnp.where(mine, total_real, 0.0), 0)
    correction[1:2, :] = along(jnp.where(mine, total_imag, 0.0), 0)
    weights[0] = jnp.broadcast_to(total_real * scale, (n, LANES))
    weights[1] = jnp.broadcast_to(total_imag * scale, (n, LANES))

    step = 4 * OCTET
    for t in range(rows // step):
        span = slice(t * step, (t + 1) * step)
        sum_real = jnp.zeros((step, LANES), F32)
        sum_imag = jnp.zeros((step, LANES), F32)
        for p in range(n):
            weight_real = weights[0, p : p + 1, :]
            weight_imag = weights[1, p : p + 1, :]
            part_real, part_imag = parts[p, 0, span, :], parts[p, 1, span, :]
            sum_real = sum_real + (weight_real * part_real - weight_imag * part_imag)
            sum_imag = sum_imag + (weight_real * part_imag + weight_imag * part_real)
        focused[0, 0, span, :] = sum_real
        focused[1, 0, span, :] = sum_imag


def solution(mesh):
    n = mesh.shape["tile"]

    def per_device(echoes, bin_start, bin_fraction, row_phase, column_phase, row_bin, column_bin):
        samples = echoes.shape[2]
        rows, columns = row_phase.shape[2], column_phase.shape[2]
        first, turn, last = tables(samples)
        bins = samples // LANES
        echo = echoes.reshape(2, bins, LANES)
        fold = fold_table(n)
        vmem = pl.BlockSpec(memory_space=pltpu.VMEM)
        depth = n * 2 * n // LANES
        return pl.pallas_call(
            functools.partial(kernel, n),
            out_shape=(
                jax.ShapeDtypeStruct((2, 1, rows, columns), F32),
                jax.ShapeDtypeStruct((2, 1), F32),
            ),
            in_specs=[pl.BlockSpec(memory_space=pltpu.SMEM)] + [vmem] * 10,
            out_specs=(vmem, vmem),
            scratch_shapes=[
                pltpu.VMEM((2, bins + OCTET, LANES), F32),
                pltpu.VMEM((n, 4, LANES), BF16),
                pltpu.VMEM((n, 4, LANES), BF16),
                pltpu.VMEM((n, rows, 3 * LANES), F32),
                pltpu.VMEM((n, 2, rows, columns), F32),
                pltpu.VMEM((n * 2 * OCTET, rows // OCTET * columns), BF16),
                pltpu.VMEM((depth, LANES), F32),
                pltpu.VMEM((n, depth, LANES), F32),
                pltpu.VMEM((2, n, LANES), F32),
                pltpu.SemaphoreType.DMA((n,)),
                pltpu.SemaphoreType.DMA((n,)),
                pltpu.SemaphoreType.DMA((n,)),
                pltpu.SemaphoreType.DMA((n,)),
            ],
            compiler_params=pltpu.CompilerParams(collective_id=0, has_side_effects=True),
        )(
            bin_start, echo, bin_fraction, row_phase, column_phase, row_bin, column_bin,
            jnp.asarray(first), jnp.asarray(turn), jnp.asarray(last), jnp.asarray(fold),
        )

    split = ("groups", "tile")
    in_specs = (
        P(None, split, None),
        P(split, None),
        P(None, split),
        P(None, split, None),
        P(None, split, None),
        P(None, split, None),
        P(None, split, None),
    )
    out_specs = (P(None, split, None, None), P(None, split))
    return jax.shard_map(per_device, mesh=mesh, in_specs=in_specs, out_specs=out_specs, check_vma=False)
```

time: 127 us -> 25.6 us (0.20)
  blocking collectives: 59.4 us -> 0 us
  local copies, waits for them, and re-layouts: 26 us -> 4.12 us
  matrix products: 21.3 us -> 0 us
  Pallas kernels: 0 us -> 20.6 us
  starting transfers between devices: 7.42 us -> 0 us
  waiting for transfers between devices: 5.88 us -> 0 us
  other arithmetic: 4.44 us -> 0 us
  between operations: 2.38 us -> 0.66 us
    psum x2 -> x0, blocking collectives: 59.4 us -> none  [the longest x1 29.9 us: per_device(): lax.psum((cross_real, cross_imag, energy), 'tile')]
    dot_general x22 -> x0, matrix products: 21.3 us -> none  [the longest x3 3.54 us: image_of(): jnp.tensordot(weight_imag, part_imag, 1, precision=highest)]
    pallas_call x0 -> x1, Pallas kernels: none -> 20.6 us  [per_device(): pl.pallas_call(functools.partial(kernel, n), out_shape=(jax.ShapeDtypeStr...]
    another operation x5 -> x0, local copies, waits for them, and re-layouts: 16.3 us -> none  [the longest x3 12.9 us: compress(): jnp.stack([final_real.reshape(-1, samples) * norm_scale, final_imag.resha...]
    all_to_all x1 -> x0, starting transfers between devices: 7.42 us -> none  [per_device(): lax.all_to_all(outgoing, 'tile', split_axis=1, concat_axis=0, tiled=True)]
    all_to_all x1 -> x0, waiting for transfers between devices: 5.88 us -> none  [per_device(): lax.all_to_all(outgoing, 'tile', split_axis=1, concat_axis=0, tiled=True)]
    gather x3 -> x0, local copies, waits for them, and re-layouts: 5.26 us -> none  [cut_window(): return lax.dynamic_slice_in_dim(profile, offset, window_len, 1)]
    slice x3 -> x0, local copies, waits for them, and re-layouts: 2.47 us -> none  [the longest x2 1.59 us: contribution(): repeated = jnp.tile(profile, (1, 1, BINR + 1))[..., :BINR * (length + 1)]]
  transfers between devices with their start and end apart: 1 -> 0, of which waited for: 1 -> 0; matrix products, arithmetic and copies ran while one was open for 0% -> 0% of each run, Pallas kernels for 0% -> 0%
where the time goes in v1:
time: 25.6 us; the launch traced here: 25.4 us
  Pallas kernels  20.6 us (80%)
  local copies, waits for them, and re-layouts  4.12 us (16%)
  between operations  0.66 us (3%)
    pallas_call x1, Pallas kernels, per_device(): pl.pallas_call(functools.partial(kernel, n), out_shape=(jax.ShapeDtypeStr...  20.6 us
    unnamed x6, local copies, waits for them, and re-layouts  3.53 us
    pallas_call x1, local copies, waits for them, and re-layouts, per_device(): pl.pallas_call(functools.partial(kernel, n), out_shape=(jax.ShapeDtypeStr...  0.6 us

profile of v1, /device:TPU:0, one launch (start us, length us, event | category | flops | bytes accessed | tf_op | source)
XLA Modules:
  0.0 25.4 jit_solution(1882393687637257610)
XLA Ops:
  0.6 0.0 copy-start
  0.6 0.6 %copy-done = f32[16,1]{0,1:T(1,128)S(1)} copy-done((f32[16,1]{0,1:T(1,128)S(1)}, f32[16,1]{0,1:T(1,128)}, u32[]{:S(2)}) %copy-start) | copy-done | bytes 88
  1.3 0.7 %copy.13.fraction = f32[16,1]{1,0:T(8,128)} copy(f32[16,1]{0,1:T(1,128)S(1)} %copy-done) | data formatting | bytes 128 | tf_op args[2]
  2.0 20.6 %shard_map.122 = (f32[2,1,128,128]{3,2,1,0:T(8,128)}, f32[2,1]{1,0:T(2,128)}) custom-call(s32[1,16]{1,0:T(1,128)} %starts.1, f32[2,128,128]{2,1,0:T(8,128)} %bitcast.1, f32[16,1]{1,0:T(8,128)} %copy.13.fraction, f32[16,1,128]{2,1,0:T(1,128)} %row_phase.1, f32[16,1,128]{2,1,0:T(1,128)} %column_phase.1, s32[16,1,128]{2,1,0:T(1,128)} %row_bin.1, ...), custom_call_target="tpu_custom_call" | custom-call | tf_op jit(solution)/shard_map/pallas_call | solution.py:280
  22.6 0.0 copy-start.1
  22.6 0.6 %copy-done.1 = f32[2,1]{1,0:T(2,128)S(1)} copy-done((f32[2,1]{1,0:T(2,128)S(1)}, f32[2,1]{1,0:T(2,128)}, u32[]{:S(2)}) %copy-start.1) | copy-done | bytes 32
  23.2 0.6 %copy.14 = f32[2,1]{0,1:T(1,128)} copy(f32[2,1]{1,0:T(2,128)S(1)} %copy-done.1) | data formatting | bytes 16 | tf_op jit(solution)/shard_map/pallas_call | solution.py:280
  23.8 1.6 %copy.16 = f32[2,1,128,128]{3,2,1,0:T(8,128)} copy(f32[2,1,128,128]{3,2,1,0:T(8,128)} %get-tuple-element.6) | data formatting | bytes 262144
Async XLA Ops:
  0.6 0.7 %copy-start = (f32[16,1]{0,1:T(1,128)S(1)}, f32[16,1]{0,1:T(1,128)}, u32[]{:S(2)}) copy-start(f32[16,1]{0,1:T(1,128)} %param.13) | copy-start | bytes 196
  22.6 0.6 %copy-start.1 = (f32[2,1]{1,0:T(2,128)S(1)}, f32[2,1]{1,0:T(2,128)}, u32[]{:S(2)}) copy-start(f32[2,1]{1,0:T(2,128)} %get-tuple-element.3) | copy-start | bytes 28

commit v2 on v1

--- a/solution.py
+++ b/solution.py
@@ -167,7 +167,7 @@
         moved = pltpu.roll(window, LANES - 1, 1)
         below = jnp.concatenate([moved[1:4], moved[0:1]], 0)
         shifted = jnp.where(lane4 == LANES - 1, below, moved)
-        share = fraction[p : p + 1, 0:1]
+        share = fraction[0, p]
         profile = ((1.0 - share) * window + share * shifted).astype(BF16).astype(F32)
         index = steer[p, :, 2 * LANES :].astype(jnp.int32)
         low = index < LANES
@@ -245,8 +245,9 @@
     total_real = one_real * two_real - one_imag * two_imag
     total_imag = one_real * two_imag + one_imag * two_real
     mine = lax.broadcasted_iota(jnp.int32, total_real.shape, 0) == me
-    correction[0:1, :] = along(jnp.where(mine, total_real, 0.0), 0)
-    correction[1:2, :] = along(jnp.where(mine, total_imag, 0.0), 0)
+    own_real = along(jnp.where(mine, total_real, 0.0), 0)
+    own_imag = along(jnp.where(mine, total_imag, 0.0), 0)
+    correction[...] = jnp.concatenate([own_real, own_imag], 1)
     weights[0] = jnp.broadcast_to(total_real * scale, (n, LANES))
     weights[1] = jnp.broadcast_to(total_imag * scale, (n, LANES))
 
@@ -277,13 +278,13 @@
         fold = fold_table(n)
         vmem = pl.BlockSpec(memory_space=pltpu.VMEM)
         depth = n * 2 * n // LANES
-        return pl.pallas_call(
+        focused, correction = pl.pallas_call(
             functools.partial(kernel, n),
             out_shape=(
-                jax.ShapeDtypeStruct((2, 1, rows, columns), F32),
-                jax.ShapeDtypeStruct((2, 1), F32),
+                pltpu.VMEM((2, 1, rows, columns), F32),
+                pltpu.VMEM((1, 2), F32),
             ),
-            in_specs=[pl.BlockSpec(memory_space=pltpu.SMEM)] + [vmem] * 10,
+            in_specs=[pl.BlockSpec(memory_space=pltpu.SMEM), vmem, pl.BlockSpec(memory_space=pltpu.SMEM)] + [vmem] * 8,
             out_specs=(vmem, vmem),
             scratch_shapes=[
                 pltpu.VMEM((2, bins + OCTET, LANES), F32),
@@ -302,9 +303,10 @@
             ],
             compiler_params=pltpu.CompilerParams(collective_id=0, has_side_effects=True),
         )(
-            bin_start, echo, bin_fraction, row_phase, column_phase, row_bin, column_bin,
+            bin_start, echo, bin_fraction.T, row_phase, column_phase, row_bin, column_bin,
             jnp.asarray(first), jnp.asarray(turn), jnp.asarray(last), jnp.asarray(fold),
         )
+        return focused, correction.T
 
     split = ("groups", "tile")
     in_specs = (

time: 25.6 us -> 21.9 us (0.86)
  local copies, waits for them, and re-layouts: 4.12 us -> 1.17 us
  Pallas kernels: 20.6 us -> 19.9 us
    unnamed x6 -> x2, local copies, waits for them, and re-layouts: 3.53 us -> 1.17 us
    pallas_call x1, Pallas kernels: 20.6 us -> 19.9 us  [per_device(): pl.pallas_call(functools.partial(kernel, n), out_shape=(pltpu.VMEM((2, 1,...]
    pallas_call x1 -> x0, local copies, waits for them, and re-layouts: 0.6 us -> none  [per_device(): pl.pallas_call(functools.partial(kernel, n), out_shape=(jax.ShapeDtypeStr...]
where the time goes in v2:
time: 21.9 us; the launch traced here: 21.7 us
  Pallas kernels  19.9 us (91%)
  local copies, waits for them, and re-layouts  1.17 us (5%)
  between operations  0.64 us (3%)
    pallas_call x1, Pallas kernels, per_device(): pl.pallas_call(functools.partial(kernel, n), out_shape=(pltpu.VMEM((2, 1,...  19.9 us
    unnamed x2, local copies, waits for them, and re-layouts  1.17 us

profile of v2, /device:TPU:0, one launch (start us, length us, event | category | flops | bytes accessed | tf_op | source)
XLA Modules:
  0.0 21.7 jit_solution(16439996734022962067)
XLA Ops:
  0.6 19.9 %shard_map.122 = (f32[2,1,128,128]{3,2,1,0:T(8,128)S(1)}, f32[1,2]{1,0:T(1,128)S(1)}) custom-call(s32[1,16]{1,0:T(1,128)} %starts.1, f32[2,128,128]{2,1,0:T(8,128)} %bitcast.4, f32[1,16]{1,0:T(1,128)} %bitcast.5, f32[16,1,128]{2,1,0:T(1,128)} %row_phase.1, f32[16,1,128]{2,1,0:T(1,128)} %column_phase.1, s32[16,1,128]{2,1,0:T(1,128)} %row_bin.1, ...), custom_call_target="tpu_custom_call" | custom-call | tf_op jit(solution)/shard_map/pallas_call | solution.py:281
  20.6 0.7 %copy.15 = f32[2,1,128,128]{3,2,1,0:T(8,128)} copy(f32[2,1,128,128]{3,2,1,0:T(8,128)S(1)} %get-tuple-element.6) | data formatting | bytes 262144
  21.2 0.5 %copy.16 = f32[2,1]{0,1:T(1,128)} copy(f32[2,1]{0,1:T(1,128)S(1)} %bitcast.3) | data formatting | bytes 16

commit v3 on v2

--- a/solution.py
+++ b/solution.py
@@ -66,8 +66,10 @@
 
 
 def kernel(
-    n, starts, echo, fraction, row_phase, column_phase, row_bin, column_bin, first, turn, last, fold,
+    n, starts_in, echo_in, first_in, turn_in, last_in, row_phase_in, column_phase_in, row_bin_in, column_bin_in,
+    fraction_in, fold_in,
     focused, correction,
+    starts, echo, first, turn, last, row_phase, column_phase, row_bin, column_bin, fraction, fold, in_sem,
     spec, outgoing, gathered, steer, parts, gram_in, message, messages, weights,
     send_sem, recv_sem, send_sem2, recv_sem2,
 ):
@@ -79,12 +81,35 @@
     for k in range(1, n):
         pl.semaphore_signal(barrier, inc=1, device_id={"tile": lax.rem(me + k, n)}, device_id_type=MESH)
 
+    sources = (
+        starts_in, echo_in, first_in, turn_in, last_in, row_phase_in, column_phase_in, row_bin_in, column_bin_in,
+        fraction_in, fold_in,
+    )
+    targets = (starts, echo, first, turn, last, row_phase, column_phase, row_bin, column_bin, fraction, fold)
+    loads = [
+        pltpu.make_async_copy(source, target, in_sem.at[i])
+        for i, (source, target) in enumerate(zip(sources, targets))
+    ]
+    for load in loads[1:] + loads[:1]:
+        load.start()
+
+    upper = (2 * me) // n
+
+    def other(k):
+        place = upper * k + (1 - upper) * (n - 2 - k)
+        return place + (place >= me).astype(jnp.int32)
+
+
+    loads[1].wait()
+    loads[2].wait()
     real, imag = echo[0], echo[1]
     data = jnp.concatenate(
         [jnp.concatenate([real, imag], 1), jnp.concatenate([imag, -real], 1)], 0
     )
     section = split3(first, data, ((1,), (0,)))
     half = section.shape[1] // 2
+    loads[3].wait()
+    loads[4].wait()
     real, imag = section[:, :half], section[:, half:]
     turned_real = real * turn[0] + imag * turn[1]
     turned_imag = imag * turn[0] - real * turn[1]
@@ -99,6 +124,7 @@
         spec[h, bins:, :] = jnp.zeros((spec.shape[1] - bins, LANES), F32)
 
     lane = lax.broadcasted_iota(jnp.int32, (OCTET, LANES), 1)
+    loads[0].wait()
     for t in range(n):
         start = starts[0, t]
         top = start // LANES
@@ -112,25 +138,25 @@
 
     pl.semaphore_wait(barrier, n - 1)
 
-    def window_copy(k):
-        target = lax.rem(me + k, n)
+    def window_copy(device, slot):
         return pltpu.make_async_remote_copy(
-            src_ref=outgoing.at[target],
-            dst_ref=gathered.at[me],
-            send_sem=send_sem.at[k],
-            recv_sem=recv_sem.at[k],
-            device_id={"tile": target},
+            src_ref=outgoing.at[device],
+            dst_ref=gathered.at[slot],
+            send_sem=send_sem.at[device],
+            recv_sem=recv_sem.at[slot],
+            device_id={"tile": device},
             device_id_type=MESH,
         )
 
-    copies = [window_copy(k) for k in range(1, n)]
-    for copy in copies:
-        copy.start()
+    for k in range(n - 1):
+        window_copy(other(k), me).start()
     gathered[me] = outgoing[me]
 
     def rounded(values):
         return values.astype(BF16).astype(F32)
 
+    for load in loads[5:]:
+        load.wait()
     angles = row_phase[:, 0, :]
     left_side = jnp.concatenate(
         [
@@ -158,11 +184,9 @@
     for p in range(n):
         steer[p] = dot(left_side, jnp.where(owner == p, right_side, 0.0).astype(BF16))
 
-    for copy in copies:
-        copy.wait()
-
     lane4 = lax.broadcasted_iota(jnp.int32, (4, LANES), 1)
-    for p in range(n):
+
+    def contribute(p):
         window = gathered[p].astype(F32)
         moved = pltpu.roll(window, LANES - 1, 1)
         below = jnp.concatenate([moved[1:4], moved[0:1]], 0)
@@ -184,11 +208,21 @@
         part_imag = turn_real * imag + turn_imag * real
         parts[p, 0] = part_real
         parts[p, 1] = part_imag
+        own_rows = pl.ds(pl.multiple_of(p * 2 * OCTET, 2 * OCTET), 2 * OCTET)
         for t in range(rows // OCTET):
             pair = jnp.concatenate(
                 [part_real[t * OCTET : (t + 1) * OCTET], part_imag[t * OCTET : (t + 1) * OCTET]], 0
             )
-            gram_in[p * 2 * OCTET : (p + 1) * 2 * OCTET, t * LANES : (t + 1) * LANES] = pair.astype(BF16)
+            gram_in[own_rows, t * LANES : (t + 1) * LANES] = pair.astype(BF16)
+
+    contribute(me)
+    near_first = [other(k) for k in reversed(range(n - 1))]
+    cuts = [0, n // 2 - 1, 3 * n // 4 - 1, n - 1]
+    for begin, end in zip(cuts[:-1], cuts[1:]):
+        for device in near_first[begin:end]:
+            window_copy(device, device).wait()
+        for device in near_first[begin:end]:
+            contribute(device)
 
     values = gram_in[...]
     product = dot(values, values, ((1,), (1,)))
@@ -206,21 +240,20 @@
     message[...] = packed
     messages[me] = packed
 
-    def gram_copy(k):
+    def gram_copy(device, slot):
         return pltpu.make_async_remote_copy(
             src_ref=message,
-            dst_ref=messages.at[me],
-            send_sem=send_sem2.at[k],
-            recv_sem=recv_sem2.at[k],
-            device_id={"tile": lax.rem(me + k, n)},
+            dst_ref=messages.at[slot],
+            send_sem=send_sem2.at[device],
+            recv_sem=recv_sem2.at[slot],
+            device_id={"tile": device},
             device_id_type=MESH,
         )
 
-    copies = [gram_copy(k) for k in range(1, n)]
-    for copy in copies:
-        copy.start()
-    for copy in copies:
-        copy.wait()
+    for k in range(n - 1):
+        gram_copy(other(k), me).start()
+    for device in near_first:
+        gram_copy(device, device).wait()
 
     total = jnp.sum(messages[...], axis=0)
     gram = jnp.concatenate(
@@ -277,6 +310,10 @@
         echo = echoes.reshape(2, bins, LANES)
         fold = fold_table(n)
         vmem = pl.BlockSpec(memory_space=pltpu.VMEM)
+        operands = (
+            bin_start, echo, jnp.asarray(first), jnp.asarray(turn), jnp.asarray(last),
+            row_phase, column_phase, row_bin, column_bin, bin_fraction.T, jnp.asarray(fold),
+        )
         depth = n * 2 * n // LANES
         focused, correction = pl.pallas_call(
             functools.partial(kernel, n),
@@ -284,9 +321,12 @@
                 pltpu.VMEM((2, 1, rows, columns), F32),
                 pltpu.VMEM((1, 2), F32),
             ),
-            in_specs=[pl.BlockSpec(memory_space=pltpu.SMEM), vmem, pl.BlockSpec(memory_space=pltpu.SMEM)] + [vmem] * 8,
+            in_specs=[pl.BlockSpec(memory_space=pltpu.HBM)] * len(operands),
             out_specs=(vmem, vmem),
-            scratch_shapes=[
+            scratch_shapes=[pltpu.SMEM(bin_start.shape, jnp.int32)]
+            + [pltpu.VMEM(operand.shape, operand.dtype) for operand in operands[1:9]]
+            + [pltpu.SMEM((1, n), F32), pltpu.VMEM(fold.shape, F32), pltpu.SemaphoreType.DMA((len(operands),))]
+            + [
                 pltpu.VMEM((2, bins + OCTET, LANES), F32),
                 pltpu.VMEM((n, 4, LANES), BF16),
                 pltpu.VMEM((n, 4, LANES), BF16),
@@ -302,10 +342,7 @@
                 pltpu.SemaphoreType.DMA((n,)),
             ],
             compiler_params=pltpu.CompilerParams(collective_id=0, has_side_effects=True),
-        )(
-            bin_start, echo, bin_fraction.T, row_phase, column_phase, row_bin, column_bin,
-            jnp.asarray(first), jnp.asarray(turn), jnp.asarray(last), jnp.asarray(fold),
-        )
+        )(*operands)
         return focused, correction.T
 
     split = ("groups", "tile")

time: 21.9 us -> 20.3 us (0.927)
  Pallas kernels: 19.9 us -> 18.3 us
    pallas_call x1, Pallas kernels: 19.9 us -> 18.3 us  [per_device(): pl.pallas_call(functools.partial(kernel, n), out_shape=(pltpu.VMEM((2, 1,...]
where the time goes in v3:
time: 20.3 us; the launch traced here: 20.1 us
  Pallas kernels  18.3 us (90%)
  local copies, waits for them, and re-layouts  1.17 us (6%)
  between operations  0.64 us (3%)
    pallas_call x1, Pallas kernels, per_device(): pl.pallas_call(functools.partial(kernel, n), out_shape=(pltpu.VMEM((2, 1,...  18.3 us
    unnamed x2, local copies, waits for them, and re-layouts  1.17 us

profile of v3, /device:TPU:0, one launch (start us, length us, event | category | flops | bytes accessed | tf_op | source)
XLA Modules:
  0.0 20.1 jit_solution(8065567387567028281)
XLA Ops:
  0.6 18.3 %shard_map.122 = (f32[2,1,128,128]{3,2,1,0:T(8,128)S(1)}, f32[1,2]{1,0:T(1,128)S(1)}) custom-call(s32[1,16]{1,0:T(1,128)} %starts_in.1, f32[2,128,128]{2,1,0:T(8,128)} %bitcast.4, bf16[2,128,256]{2,1,0:T(8,128)(2,1)} %constant.6.clone.first_in.last_in, f32[2,128,128]{2,1,0:T(8,128)} %constant.7.clone.turn_in, ...), custom_call_target="tpu_custom_call" | custom-call | tf_op jit(solution)/shard_map/pallas_call | solution.py:318
  18.9 0.7 %copy.15 = f32[2,1,128,128]{3,2,1,0:T(8,128)} copy(f32[2,1,128,128]{3,2,1,0:T(8,128)S(1)} %get-tuple-element.6) | data formatting | bytes 262144
  19.6 0.5 %copy.16 = f32[2,1]{0,1:T(1,128)} copy(f32[2,1]{0,1:T(1,128)S(1)} %bitcast.3) | data formatting | bytes 16

commit v4 on v3

--- a/solution.py
+++ b/solution.py
@@ -68,9 +68,9 @@
 def kernel(
     n, starts_in, echo_in, first_in, turn_in, last_in, row_phase_in, column_phase_in, row_bin_in, column_bin_in,
     fraction_in, fold_in,
-    focused, correction,
+    parts, weights, correction,
     starts, echo, first, turn, last, row_phase, column_phase, row_bin, column_bin, fraction, fold, in_sem,
-    spec, outgoing, gathered, steer, parts, gram_in, message, messages, weights,
+    spec, outgoing, gathered, steer, gram_in, message, messages,
     send_sem, recv_sem, send_sem2, recv_sem2,
 ):
     me = lax.axis_index("tile")
@@ -93,12 +93,22 @@
     for load in loads[1:] + loads[:1]:
         load.start()
 
-    upper = (2 * me) // n
-
-    def other(k):
-        place = upper * k + (1 - upper) * (n - 2 - k)
-        return place + (place >= me).astype(jnp.int32)
-
+    block = math.gcd(n, 4)
+    here, upper = me // block, (2 * me) // n
+
+    def within(i):
+        place = 0
+        for bit in (1, 2):
+            if bit < block:
+                place = place + lax.rem(lax.rem(me // bit, 2) + (i // bit) % 2, 2) * bit
+        return place
+
+    near_first = [here * block + within(i) for i in range(1, block)]
+    for k in range(n // block - 1):
+        place = upper * (n // block - 2 - k) + (1 - upper) * k
+        place = place + (place >= here).astype(jnp.int32)
+        near_first += [place * block + within(i) for i in range(block)]
+    far_first = near_first[::-1]
 
     loads[1].wait()
     loads[2].wait()
@@ -148,8 +158,8 @@
             device_id_type=MESH,
         )
 
-    for k in range(n - 1):
-        window_copy(other(k), me).start()
+    for device in far_first:
+        window_copy(device, me).start()
     gathered[me] = outgoing[me]
 
     def rounded(values):
@@ -216,8 +226,7 @@
             gram_in[own_rows, t * LANES : (t + 1) * LANES] = pair.astype(BF16)
 
     contribute(me)
-    near_first = [other(k) for k in reversed(range(n - 1))]
-    cuts = [0, n // 2 - 1, 3 * n // 4 - 1, n - 1]
+    cuts = [0, n // 2 - 1, n - 5, n - 3, n - 1]
     for begin, end in zip(cuts[:-1], cuts[1:]):
         for device in near_first[begin:end]:
             window_copy(device, device).wait()
@@ -250,8 +259,8 @@
             device_id_type=MESH,
         )
 
-    for k in range(n - 1):
-        gram_copy(other(k), me).start()
+    for device in far_first:
+        gram_copy(device, me).start()
     for device in near_first:
         gram_copy(device, device).wait()
 
@@ -284,9 +293,14 @@
     weights[0] = jnp.broadcast_to(total_real * scale, (n, LANES))
     weights[1] = jnp.broadcast_to(total_imag * scale, (n, LANES))
 
+
+def finish(parts, weights, own, focused, correction, image, sem):
+    n, rows = parts.shape[0], parts.shape[2]
     step = 4 * OCTET
+    stores = [pltpu.make_async_copy(own, correction, sem.at[0])]
+    stores[0].start()
     for t in range(rows // step):
-        span = slice(t * step, (t + 1) * step)
+        span = pl.ds(t * step, step)
         sum_real = jnp.zeros((step, LANES), F32)
         sum_imag = jnp.zeros((step, LANES), F32)
         for p in range(n):
@@ -295,8 +309,14 @@
             part_real, part_imag = parts[p, 0, span, :], parts[p, 1, span, :]
             sum_real = sum_real + (weight_real * part_real - weight_imag * part_imag)
             sum_imag = sum_imag + (weight_real * part_imag + weight_imag * part_real)
-        focused[0, 0, span, :] = sum_real
-        focused[1, 0, span, :] = sum_imag
+        image[0, 0, span, :] = sum_real
+        image[1, 0, span, :] = sum_imag
+        stores.append(
+            pltpu.make_async_copy(image.at[:, :, span, :], focused.at[:, :, span, :], sem.at[t + 1])
+        )
+        stores[-1].start()
+    for store in stores:
+        store.wait()
 
 
 def solution(mesh):
@@ -315,14 +335,15 @@
             row_phase, column_phase, row_bin, column_bin, bin_fraction.T, jnp.asarray(fold),
         )
         depth = n * 2 * n // LANES
-        focused, correction = pl.pallas_call(
+        parts, weights, own = pl.pallas_call(
             functools.partial(kernel, n),
             out_shape=(
-                pltpu.VMEM((2, 1, rows, columns), F32),
+                pltpu.VMEM((n, 2, rows, columns), F32),
+                pltpu.VMEM((2, n, LANES), F32),
                 pltpu.VMEM((1, 2), F32),
             ),
             in_specs=[pl.BlockSpec(memory_space=pltpu.HBM)] * len(operands),
-            out_specs=(vmem, vmem),
+            out_specs=(vmem, vmem, vmem),
             scratch_shapes=[pltpu.SMEM(bin_start.shape, jnp.int32)]
             + [pltpu.VMEM(operand.shape, operand.dtype) for operand in operands[1:9]]
             + [pltpu.SMEM((1, n), F32), pltpu.VMEM(fold.shape, F32), pltpu.SemaphoreType.DMA((len(operands),))]
@@ -331,18 +352,32 @@
                 pltpu.VMEM((n, 4, LANES), BF16),
                 pltpu.VMEM((n, 4, LANES), BF16),
                 pltpu.VMEM((n, rows, 3 * LANES), F32),
-                pltpu.VMEM((n, 2, rows, columns), F32),
                 pltpu.VMEM((n * 2 * OCTET, rows // OCTET * columns), BF16),
                 pltpu.VMEM((depth, LANES), F32),
                 pltpu.VMEM((n, depth, LANES), F32),
-                pltpu.VMEM((2, n, LANES), F32),
                 pltpu.SemaphoreType.DMA((n,)),
                 pltpu.SemaphoreType.DMA((n,)),
                 pltpu.SemaphoreType.DMA((n,)),
                 pltpu.SemaphoreType.DMA((n,)),
             ],
-            compiler_params=pltpu.CompilerParams(collective_id=0, has_side_effects=True),
+            compiler_params=pltpu.CompilerParams(
+                collective_id=0, has_side_effects=True, vmem_limit_bytes=32 << 20
+            ),
         )(*operands)
+        focused, correction = pl.pallas_call(
+            finish,
+            out_shape=(
+                jax.ShapeDtypeStruct((2, 1, rows, columns), F32),
+                jax.ShapeDtypeStruct((1, 2), F32),
+            ),
+            in_specs=[vmem] * 3,
+            out_specs=[pl.BlockSpec(memory_space=pltpu.HBM)] * 2,
+            scratch_shapes=[
+                pltpu.VMEM((2, 1, rows, columns), F32),
+                pltpu.SemaphoreType.DMA((rows // (4 * OCTET) + 1,)),
+            ],
+            compiler_params=pltpu.CompilerParams(vmem_limit_bytes=16 << 20),
+        )(*[pltpu.with_memory_space_constraint(value, pltpu.VMEM) for value in (parts, weights, own)])
         return focused, correction.T
 
     split = ("groups", "tile")

time: 20.3 us -> 27.8 us (1.37)
  local copies, waits for them, and re-layouts: 1.17 us -> 7.75 us
  Pallas kernels: 18.3 us -> 19 us
    unnamed x2 -> x20, local copies, waits for them, and re-layouts: 1.17 us -> 7.75 us
    pallas_call x1 -> x2, Pallas kernels: 18.3 us -> 19 us  [the longest x1 18 us: per_device(): pl.pallas_call(functools.partial(kernel, n), out_shape=(pltpu.VMEM((n, 2,...]
where the time goes in v4:
time: 27.8 us; the launch traced here: 27.5 us
  Pallas kernels  19 us (68%)
  local copies, waits for them, and re-layouts  7.75 us (28%)
  between operations  0.66 us (2%)
    pallas_call x1, Pallas kernels, per_device(): pl.pallas_call(functools.partial(kernel, n), out_shape=(pltpu.VMEM((n, 2,...  18 us
    unnamed x20, local copies, waits for them, and re-layouts  7.75 us
    pallas_call x1, Pallas kernels, per_device(): pl.pallas_call(finish, out_shape=(jax.ShapeDtypeStruct((2, 1, rows, colum...  1.05 us

profile of v4, /device:TPU:0, one launch (start us, length us, event | category | flops | bytes accessed | tf_op | source)
XLA Modules:
  0.0 27.5 jit_solution(16219856542703104565)
XLA Ops:
  0.6 0.0 copy-start
  0.6 0.9 %copy-done = bf16[2,128,256]{2,1,0:T(8,128)(2,1)S(1)} copy-done((bf16[2,128,256]{2,1,0:T(8,128)(2,1)S(1)}, bf16[2,128,256]{2,1,0:T(8,128)(2,1)}, u32[]{:S(2)}) %copy-start) | copy-done | bytes 131096
  1.5 0.0 copy-start.1
  1.5 0.9 %copy-done.1 = f32[2,256,128]{2,1,0:T(8,128)S(1)} copy-done((f32[2,256,128]{2,1,0:T(8,128)S(1)}, f32[2,256,128]{2,1,0:T(8,128)}, u32[]{:S(2)}) %copy-start.1) | copy-done | bytes 262168
  2.5 0.0 copy-start.2
  2.5 0.9 %copy-done.2 = f32[2,1,16384]{2,1,0:T(1,128)S(1)} copy-done((f32[2,1,16384]{2,1,0:T(1,128)S(1)}, f32[2,1,16384]{2,1,0:T(1,128)}, u32[]{:S(2)}) %copy-start.2) | copy-done | bytes 131096
  3.4 0.0 copy-start.3
  3.4 0.9 %copy-done.3 = f32[2,128,128]{2,1,0:T(8,128)S(1)} copy-done((f32[2,128,128]{2,1,0:T(8,128)S(1)}, f32[2,128,128]{2,1,0:T(8,128)}, u32[]{:S(2)}) %copy-start.3) | copy-done | bytes 131096
  4.3 0.0 copy-start.4
  4.3 0.7 %copy-done.4 = f32[16,1,128]{2,1,0:T(1,128)S(1)} copy-done((f32[16,1,128]{2,1,0:T(1,128)S(1)}, f32[16,1,128]{2,1,0:T(1,128)}, u32[]{:S(2)}) %copy-start.4) | copy-done | bytes 8216
  5.0 0.0 copy-start.5
  5.0 0.7 %copy-done.5 = f32[16,1,128]{2,1,0:T(1,128)S(1)} copy-done((f32[16,1,128]{2,1,0:T(1,128)S(1)}, f32[16,1,128]{2,1,0:T(1,128)}, u32[]{:S(2)}) %copy-start.5) | copy-done | bytes 8216
  5.7 0.0 copy-start.6
  5.7 0.7 %copy-done.6 = s32[16,1,128]{2,1,0:T(1,128)S(1)} copy-done((s32[16,1,128]{2,1,0:T(1,128)S(1)}, s32[16,1,128]{2,1,0:T(1,128)}, u32[]{:S(2)}) %copy-start.6) | copy-done | bytes 8216
  6.4 0.0 copy-start.7
  6.4 0.7 %copy-done.7 = s32[16,1,128]{2,1,0:T(1,128)S(1)} copy-done((s32[16,1,128]{2,1,0:T(1,128)S(1)}, s32[16,1,128]{2,1,0:T(1,128)}, u32[]{:S(2)}) %copy-start.7) | copy-done | bytes 8216
  7.1 0.0 copy-start.8
  7.1 0.7 %copy-done.8 = s32[1,16]{1,0:T(1,128)S(1)} copy-done((s32[1,16]{1,0:T(1,128)S(1)}, s32[1,16]{1,0:T(1,128)}, u32[]{:S(2)}) %copy-start.8) | copy-done | bytes 88
  7.7 0.0 copy-start.9
  7.7 0.7 %copy-done.9 = f32[16,1]{0,1:T(1,128)S(1)} copy-done((f32[16,1]{0,1:T(1,128)S(1)}, f32[16,1]{0,1:T(1,128)}, u32[]{:S(2)}) %copy-start.9) | copy-done | bytes 88
  8.4 18.0 %shard_map.122 = (f32[16,2,128,128]{3,2,1,0:T(8,128)S(1)}, f32[2,16,128]{2,1,0:T(8,128)S(1)}, f32[1,2]{1,0:T(1,128)S(1)}) custom-call(s32[1,16]{1,0:T(1,128)S(1)} %copy-done.8, f32[2,128,128]{2,1,0:T(8,128)S(1)} %bitcast.3, bf16[2,128,256]{2,1,0:T(8,128)(2,1)S(1)} %copy-done, f32[2,128,128]{2,1,0:T(8,128)S(1)} %copy-done.3, ...), custom_call_target="tpu_custom_call" | custom-call | tf_op jit(solution)/shard_map/pallas_call | solution.py:338
  26.4 1.0 %shard_map.123 = (f32[2,1,128,128]{3,2,1,0:T(8,128)}, f32[1,2]{1,0:T(1,128)}) custom-call(f32[16,2,128,128]{3,2,1,0:T(8,128)S(1)} %get-tuple-element.7.parts, f32[2,16,128]{2,1,0:T(8,128)S(1)} %get-tuple-element.8.weights, f32[1,2]{1,0:T(1,128)S(1)} %get-tuple-element.9.own), custom_call_target="tpu_custom_call" | custom-call | tf_op jit(solution)/shard_map/pallas_call | solution.py:367
Async XLA Ops:
  0.6 0.9 %copy-start = (bf16[2,128,256]{2,1,0:T(8,128)(2,1)S(1)}, bf16[2,128,256]{2,1,0:T(8,128)(2,1)}, u32[]{:S(2)}) copy-start(bf16[2,128,256]{2,1,0:T(8,128)(2,1)} %constant.6.clone.first_in.last_in) | copy-start | bytes 393220
  1.5 0.9 %copy-start.1 = (f32[2,256,128]{2,1,0:T(8,128)S(1)}, f32[2,256,128]{2,1,0:T(8,128)}, u32[]{:S(2)}) copy-start(f32[2,256,128]{2,1,0:T(8,128)} %constant.8.clone.fold_in) | copy-start | bytes 786436
  2.5 0.9 %copy-start.2 = (f32[2,1,16384]{2,1,0:T(1,128)S(1)}, f32[2,1,16384]{2,1,0:T(1,128)}, u32[]{:S(2)}) copy-start(f32[2,1,16384]{2,1,0:T(1,128)} %param.11) | copy-start | bytes 393220
  3.4 0.9 %copy-start.3 = (f32[2,128,128]{2,1,0:T(8,128)S(1)}, f32[2,128,128]{2,1,0:T(8,128)}, u32[]{:S(2)}) copy-start(f32[2,128,128]{2,1,0:T(8,128)} %constant.7.clone.turn_in) | copy-start | bytes 393220
  4.3 0.7 %copy-start.4 = (f32[16,1,128]{2,1,0:T(1,128)S(1)}, f32[16,1,128]{2,1,0:T(1,128)}, u32[]{:S(2)}) copy-start(f32[16,1,128]{2,1,0:T(1,128)} %row_phase_in.1) | copy-start | bytes 24580
  5.0 0.7 %copy-start.5 = (f32[16,1,128]{2,1,0:T(1,128)S(1)}, f32[16,1,128]{2,1,0:T(1,128)}, u32[]{:S(2)}) copy-start(f32[16,1,128]{2,1,0:T(1,128)} %column_phase_in.1) | copy-start | bytes 24580
  5.7 0.7 %copy-start.6 = (s32[16,1,128]{2,1,0:T(1,128)S(1)}, s32[16,1,128]{2,1,0:T(1,128)}, u32[]{:S(2)}) copy-start(s32[16,1,128]{2,1,0:T(1,128)} %row_bin_in.1) | copy-start | bytes 24580
  6.4 0.7 %copy-start.7 = (s32[16,1,128]{2,1,0:T(1,128)S(1)}, s32[16,1,128]{2,1,0:T(1,128)}, u32[]{:S(2)}) copy-start(s32[16,1,128]{2,1,0:T(1,128)} %column_bin_in.1) | copy-start | bytes 24580
  7.1 0.7 %copy-start.8 = (s32[1,16]{1,0:T(1,128)S(1)}, s32[1,16]{1,0:T(1,128)}, u32[]{:S(2)}) copy-start(s32[1,16]{1,0:T(1,128)} %starts_in.1) | copy-start | bytes 196
  7.7 0.7 %copy-start.9 = (f32[16,1]{0,1:T(1,128)S(1)}, f32[16,1]{0,1:T(1,128)}, u32[]{:S(2)}) copy-start(f32[16,1]{0,1:T(1,128)} %param.13) | copy-start | bytes 196
